TPU v7x, 32 devices: a 4x4x1 block of a 4x4x8 slice. The times are simulated.
32 devices in a mesh: rep: 1 (over z), dp: 32 (over x, y, core).
Axes of the slice: x: 4, y: 4, z: 1, core: 2. Of those that a mesh axis runs over, the one named last changes fastest.
The devices are a block of a 4x4x8 slice.
Arguments:
- x: bfloat16 [32, 2048, 768], P(('rep', 'dp'))
- dy: bfloat16 [32, 2048, 768], P(('rep', 'dp'))
- w_gate: bfloat16 [2, 768, 2304], replicated
- w_up: bfloat16 [2, 768, 2304], replicated
- w_down: bfloat16 [2, 2304, 768], replicated
- m_w_gate: float32 [2, 768, 2304], replicated
- m_w_up: float32 [2, 768, 2304], replicated
- m_w_down: float32 [2, 2304, 768], replicated
- v_w_gate: float32 [2, 768, 2304], replicated
- v_w_up: float32 [2, 768, 2304], replicated
- v_w_down: float32 [2, 2304, 768], replicated
Outputs:
- output 1: bfloat16 [2, 768, 2304], P('rep')
- output 2: bfloat16 [2, 768, 2304], P('rep')
- output 3: bfloat16 [2, 2304, 768], P('rep')
- output 4: float32 [2, 768, 2304], P('rep')
- output 5: float32 [2, 768, 2304], P('rep')
- output 6: float32 [2, 2304, 768], P('rep')
- output 7: float32 [2, 768, 2304], P('rep')
- output 8: float32 [2, 768, 2304], P('rep')
- output 9: float32 [2, 2304, 768], P('rep')
All inputs are finite; a program needn't handle non-finite values.
Results may differ from a plain program's by a relative error of at most 0.02.
Values are sent between devices in bfloat16 or wider.
A program may use at most 768 MiB of HBM per device.

v0:
```python
import jax
import jax.numpy as jnp
from jax import lax
from jax.sharding import PartitionSpec as P

NAMES = ("w_gate", "w_up", "w_down")


def matmul(a, w):
    return jnp.dot(a, w, preferred_element_type=jnp.float32).astype(jnp.bfloat16)


def normed(h):
    wide = h.astype(jnp.float32)
    scale = lax.rsqrt(jnp.mean(wide**2, -1, keepdims=True) + 1e-6)
    return (wide * scale).astype(jnp.bfloat16)


def layer(h, w):
    a = normed(h)
    gate = jnp.dot(a, w["w_gate"], preferred_element_type=jnp.float32)
    up = jnp.dot(a, w["w_up"], preferred_element_type=jnp.float32)
    return h + matmul((jax.nn.silu(gate) * up).astype(jnp.bfloat16), w["w_down"])


def adamw(w, m, v, g):
    m = 0.9 * m + 0.1 * g
    v = 0.95 * v + 0.05 * g * g
    step = m * lax.rsqrt(v + 1e-8) + 0.1 * w
    return (w - 0.02 * step).astype(jnp.bfloat16), m, v


def solution(mesh):
    def step(x, dy, *arrays):
        weights, m, v = (arrays[i : i + 3] for i in (0, 3, 6))
        layers = weights[0].shape[0]
        h, kept = x[0], []
        for number in range(layers):
            kept.append(h)
            h = layer(h, {name: w[number] for name, w in zip(NAMES, weights, strict=True)})
        by_h, summed = dy[0], [None] * layers
        for number in reversed(range(layers)):
            _, back = jax.vjp(lambda w, h: layer(h, w), {name: w[number] for name, w in zip(NAMES, weights, strict=True)}, kept[number])
            by_w, by_h = back(by_h)
            summed[number] = [lax.psum(by_w[name], "dp") for name in NAMES]
        gradients = [jnp.stack([summed[number][i] for number in range(layers)]).astype(jnp.float32) for i in range(3)]
        new = [adamw(w.astype(jnp.float32), m, v, g) for w, m, v, g in zip(weights, m, v, gradients, strict=True)]
        return tuple(one[which] for which in range(3) for one in new)

    return jax.shard_map(
        step,
        mesh=mesh,
        in_specs=(P(("rep", "dp"), None, None),) * 2 + (P(None, None, None),) * 9,
        out_specs=(P("rep", None, None),) * 9,
        check_vma=False,
    )
```

profile of v0, /device:TPU:97, one launch (start us, length us, event | category | flops | bytes accessed | tf_op | source)
XLA Modules:
  0.0 517.8 jit_solution(16352038186301998017)
XLA Ops:
  7.2 0.1 all-reduce.3.cloned.1.call-start
  7.3 3.2 copy.20
  10.5 0.0 copy-start
  10.5 0.7 fusion.30
  11.2 5.0 copy.21
  16.2 12.5 %convolution_convert_fusion.1 = bf16[2048,2304]{1,0:T(8,128)(2,1)} fusion(bf16[2,2304,768]{2,1,0:T(8,128)(2,1)} %param.15, bf16[1,2048,768]{2,1,0:T(8,128)(2,1)} %param.12), kind=kOutput, calls=%fused_computation.50 | convolution fusion | flops 7252475904 | bytes 16121856 | tf_op jit(solution)/shard_map/transpose(jvp())/dot_general | solution.py:10
  28.7 13.0 %fusion.64 = f32[2048,2304]{1,0:T(8,128)} fusion(bf16[2,768,2304]{2,1,0:T(8,128)(2,1)} %param.13, bf16[1,2048,768]{2,1,0:T(8,128)(2,1)S(1)} %copy-done.4, f32[2048]{0:T(1024)S(1)} %add_rsqrt_fusion), kind=kOutput, calls=%fused_computation.96 | convolution fusion | flops 7252475904 | bytes 25567232 | tf_op jit(solution)/shard_map/dot_general | solution.py:21
  41.7 19.0 %multiply_convert_fusion.1 = (bf16[2048,2304]{1,0:T(8,128)(2,1)}, f32[2048,2304]{1,0:T(8,128)}) fusion(f32[2048,2304]{1,0:T(8,128)} %fusion.64, bf16[2,768,2304]{2,1,0:T(8,128)(2,1)} %param.14, bf16[1,2048,768]{2,1,0:T(8,128)(2,1)} %param.11, f32[2048]{0:T(1024)S(1)} %add_rsqrt_fusion), kind=kOutput, calls=%fused_computation.20 | convolution fusion | flops 7280787456 | bytes 53878784 | tf_op jit(solution)/shard_map/dot_general | solution.py:22
  60.7 11.9 %fusion.34 = (f32[2048]{0:T(1024)S(1)}, bf16[2048,768]{0,1:T(8,128)(2,1)S(1)}) fusion(bf16[2048,2304]{1,0:T(8,128)(2,1)} %get-tuple-element.24, bf16[2,2304,768]{2,1,0:T(8,128)(2,1)} %param.15, bf16[1,2048,768]{1,2,0:T(8,128)(2,1)S(1)} %copy.20), kind=kOutput, calls=%fused_computation.67 | convolution fusion | flops 7255619584 | bytes 19275776 | tf_op jit(solution)/shard_map/dot_general | solution.py:10
  72.6 0.0 copy-start.6
  72.7 0.6 copy-done.8
  73.2 1.1 copy-done.6
  74.3 13.5 %fusion.51 = f32[2048,2304]{1,0:T(8,128)} fusion(bf16[2,768,2304]{2,1,0:T(8,128)(2,1)} %param.14, bf16[2048,768]{0,1:T(8,128)(2,1)S(1)} %get-tuple-element.27, f32[2048]{0:T(1024)S(1)} %fusion.102), kind=kOutput, calls=%fused_computation.83 | convolution fusion | flops 7252475904 | bytes 25567232 | tf_op jit(solution)/shard_map/jvp()/dot_general | solution.py:22
  87.8 30.8 %fusion.2 = (bf16[2048,2304]{1,0:T(8,128)(2,1)}, f32[2048,2304]{1,0:T(8,128)}) fusion(f32[2048,2304]{1,0:T(8,128)} %fusion.51, bf16[2048,2304]{1,0:T(8,128)(2,1)} %convolution_convert_fusion.1, bf16[2,768,2304]{2,1,0:T(8,128)(2,1)} %param.13, bf16[2048,768]{0,1:T(8,128)(2,1)} %copy-done.6, f32[2048]{0:T(1024)S(1)} %fusion.102), kind=kOutput, calls=%fused_computation.11 | convolution fusion | flops 7309099008 | bytes 63315968 | tf_op jit(solution)/shard_map/jvp()/dot_general | solution.py:21
  118.6 0.0 copy-start.7
  118.6 0.0 copy-start.12
  118.7 11.3 %fusion.72 = bf16[2048,768]{0,1:T(8,128)(2,1)} fusion(bf16[2048,2304]{1,0:T(8,128)(2,1)} %get-tuple-element.28, bf16[2,768,2304]{2,1,0:T(8,128)(2,1)S(1)} %bitcast.83), kind=kOutput, calls=%fused_computation.102 | convolution fusion | flops 7247757312 | bytes 16121856 | tf_op jit(solution)/shard_map/transpose(jvp())/dot_general | solution.py:21
  130.0 8.9 %fusion.44 = bf16[1,768,2304]{2,1,0:T(8,128)(2,1)} fusion(bf16[2048,2304]{1,0:T(8,128)(2,1)S(1)} %copy-done.12, bf16[2048,768]{0,1:T(8,128)(2,1)S(1)} %copy-done.7, f32[2048]{0:T(1024)S(1)} %fusion.102), kind=kOutput, calls=%fused_computation.78 | convolution fusion | flops 7252475904 | bytes 16130048 | tf_op jit(solution)/shard_map/transpose(jvp())/dot_general | solution.py:21
  138.9 17.8 %fusion.43 = bf16[1,2304,768]{2,1,0:T(8,128)(2,1)} fusion(f32[2048,2304]{1,0:T(8,128)} %fusion.51, bf16[1,2048,768]{2,1,0:T(8,128)(2,1)S(1)} %copy-done.5, f32[2048,2304]{1,0:T(8,128)} %get-tuple-element.29), kind=kOutput, calls=%fused_computation.77 | convolution fusion | flops 7277838336 | bytes 44433408 | tf_op jit(solution)/shard_map/transpose(jvp())/dot_general | solution.py:10
  156.7 16.4 %fusion.50 = bf16[1,768,2304]{2,1,0:T(8,128)(2,1)} fusion(bf16[2048,2304]{1,0:T(8,128)(2,1)} %convolution_convert_fusion.1, bf16[2048,768]{0,1:T(8,128)(2,1)} %copy-done.6, f32[2048]{0:T(1024)S(1)} %fusion.102, f32[2048,2304]{1,0:T(8,128)} %get-tuple-element.29), kind=kOutput, calls=%fused_computation.82 | convolution fusion | flops 7282556928 | bytes 35004416 | tf_op jit(solution)/shard_map/transpose(jvp())/dot_general | solution.py:22
  173.2 19.6 %fusion.36 = (f32[2048]{0:T(1024)S(1)}, bf16[2048,768]{0,1:T(8,128)(2,1)}) fusion(bf16[2048,768]{0,1:T(8,128)(2,1)} %copy-done.6, bf16[2048,768]{0,1:T(8,128)(2,1)} %fusion.72, bf16[2,768,2304]{2,1,0:T(8,128)(2,1)} %param.14, bf16[2048,2304]{1,0:T(8,128)(2,1)} %convolution_convert_fusion.1, f32[2048,2304]{1,0:T(8,128)} %get-tuple-element.29), kind=kOutput, calls=%fused_computation.69 | convolution fusion | flops 7285504000 | bytes 41295872 | tf_op jit(solution)/shard_map/transpose(jvp())/dot_general | solution.py:22
  192.8 0.0 slice-start
  192.8 5.2 %fusion.80 = bf16[2048,768]{0,1:T(8,128)(2,1)S(1)} fusion(bf16[2048,768]{0,1:T(8,128)(2,1)} %copy-done.6, bf16[2048,768]{0,1:T(8,128)(2,1)} %get-tuple-element.31, bf16[1,2048,768]{1,2,0:T(8,128)(2,1)S(1)} %copy-done.2, f32[2048]{0:T(1024)S(1)} %multiply_multiply_fusion.3, f32[2048]{0:T(1024)S(1)} %fusion.102), kind=kLoop, calls=%fused_computation.105 | loop fusion | flops 11010048 | bytes 12599296 | tf_op jit(solution)/shard_map/transpose(jvp())/add_any | solution.py:14
  198.0 0.0 slice-start.1
  198.0 11.6 %fusion.45 = bf16[1,2304,768]{2,1,0:T(8,128)(2,1)} fusion(bf16[2048,2304]{1,0:T(8,128)(2,1)} %get-tuple-element.24, bf16[2048,768]{0,1:T(8,128)(2,1)S(1)} %fusion.80), kind=kOutput, calls=%fused_computation.79 | convolution fusion | flops 7249526784 | bytes 16121856 | tf_op jit(solution)/shard_map/transpose(jvp())/dot_general | solution.py:10
  209.6 10.3 %convolution_convert_fusion = bf16[2048,2304]{1,0:T(8,128)(2,1)} fusion(bf16[2048,768]{0,1:T(8,128)(2,1)S(1)} %fusion.80, bf16[2,2304,768]{2,1,0:T(8,128)(2,1)S(1)} %bitcast.81), kind=kOutput, calls=%fused_computation.49 | convolution fusion | flops 7252475904 | bytes 16121856 | tf_op jit(solution)/shard_map/transpose(jvp())/dot_general | solution.py:10
  219.9 15.6 %fusion.46 = bf16[1,768,2304]{2,1,0:T(8,128)(2,1)} fusion(bf16[2048,2304]{1,0:T(8,128)(2,1)} %convolution_convert_fusion, f32[2048,2304]{1,0:T(8,128)} %fusion.64, bf16[1,2048,768]{1,2,0:T(8,128)(2,1)S(1)} %copy-done.1, f32[2048]{0:T(1024)S(1)} %copy-done.11), kind=kOutput, calls=%fused_computation.80 | convolution fusion | flops 7282556928 | bytes 35004416 | tf_op jit(solution)/shard_map/transpose(jvp())/dot_general | solution.py:22
  235.5 20.2 %fusion.47 = bf16[1,768,2304]{2,1,0:T(8,128)(2,1)} fusion(f32[2048,2304]{1,0:T(8,128)} %fusion.64, f32[2048,2304]{1,0:T(8,128)} %get-tuple-element.25, bf16[2048,2304]{1,0:T(8,128)(2,1)} %convolution_convert_fusion, bf16[1,2048,768]{1,2,0:T(8,128)(2,1)S(1)} %copy-done.1, f32[2048]{0:T(1024)S(1)} %copy-done.11), kind=kOutput, calls=%fused_computation.81 | convolution fusion | flops 7306149888 | bytes 53878784 | tf_op jit(solution)/shard_map/transpose(jvp())/dot_general | solution.py:21
  255.7 0.1 all-reduce.3.cloned.1.call-update
  255.7 182.3 %all-reduce.3.cloned.1.call-done = (bf16[1,768,2304]{2,1,0:T(8,128)(2,1)}, bf16[1,768,2304]{2,1,0:T(8,128)(2,1)}, bf16[1,768,2304]{2,1,0:T(8,128)(2,1)}, bf16[1,...) async-done(((bf16[1,768,2304]{2,1,0:T(8,128)(2,1)}, bf16[1,768,2304]{2,1,0:T(8,128)(2,1)}, bf16[1,768,2304]{2,1,0:T(8,128)(2,1)}, ...) | async-done | bytes 21233680 | tf_op jit(solution)/shard_map/psum | solution.py:45
  438.0 25.0 %fusion.21 = (bf16[2,2304,768]{2,1,0:T(8,128)(2,1)}, f32[2,2304,768]{2,1,0:T(8,128)}, f32[2,2304,768]{2,1,0:T(8,128)}) fusion(bf16[2,2304,768]{2,1,0:T(8,128)(2,1)} %param.15, bf16[1,2304,768]{2,1,0:T(8,128)(2,1)} %get-tuple-element.13, bf16[1,2304,768]{2,1,0:T(8,128)(2,1)} %get-tuple-element.14, f32[2,2304,768]{2,1,0:T(8,128)} %param.21, ...), kind=kLoop, calls=%fused_computation.42 | loop fusion | flops 67239936 | bytes 77856768 | tf_op jit(solution)/shard_map/convert_element_type | solution.py:30
  463.0 47.4 %fusion.13 = (bf16[2,768,2304]{2,1,0:T(8,128)(2,1)}, f32[2,768,2304]{2,1,0:T(8,128)}, f32[2,768,2304]{2,1,0:T(8,128)}, bf16[2,768,2304]{2,1,0:T(8,128)(2,1)}, f3...) fusion(bf16[2,768,2304]{2,1,0:T(8,128)(2,1)} %param.13, bf16[1,768,2304]{2,1,0:T(8,128)(2,1)S(1)} %copy-done.3, ...), kind=kLoop, calls=%fused_computation.34 | loop fusion | flops 134479872 | bytes 155713536 | tf_op jit(solution)/shard_map/convert_element_type | solution.py:30
  (31 shorter events, 0.1 us)
Async XLA Ops:
  7.2 430.8 %all-reduce.3.cloned.1.call-start = ((), (), s32[]{:S(2)}) async-start(), calls=%async_computation | async-start | bytes 42467328 | tf_op jit(solution)/shard_map/psum | solution.py:45
  10.5 50.2 %copy-start = (bf16[1,2048,768]{1,2,0:T(8,128)(2,1)}, bf16[1,2048,768]{1,2,0:T(8,128)(2,1)S(1)}, u32[]{:S(2)}) copy-start(bf16[1,2048,768]{1,2,0:T(8,128)(2,1)S(1)} %copy.20) | copy-start | bytes 9437188
  11.1 30.6 %copy-start.10 = (f32[2048]{0:T(1024)}, f32[2048]{0:T(1024)S(1)}, u32[]{:S(2)}) copy-start(f32[2048]{0:T(1024)S(1)} %add_rsqrt_fusion) | copy-start | bytes 24580
  16.2 12.6 %copy-start.4 = (bf16[1,2048,768]{2,1,0:T(8,128)(2,1)S(1)}, bf16[1,2048,768]{2,1,0:T(8,128)(2,1)}, u32[]{:S(2)}) copy-start(bf16[1,2048,768]{2,1,0:T(8,128)(2,1)} %param.11) | copy-start | bytes 9437188
  72.6 0.6 copy-start.8
  72.6 1.7 copy-start.6
  74.3 44.3 %slice-start.2 = ((s8[7077888]{0:T(1024)(128)(4,1)}), s8[4194304]{0:T(1024)(128)(4,1)S(1)}, s32[]{:S(2)}) async-start(s8[7077888]{0:T(1024)(128)(4,1)} %bitcast.82), calls=%async_computation.3 | async-start | bytes 8388608
  87.8 30.8 %slice-start.3 = ((s8[7077888]{0:T(1024)(128)(4,1)}), s8[2883584]{0:T(1024)(128)(4,1)S(1)}, s32[]{:S(2)}) async-start(s8[7077888]{0:T(1024)(128)(4,1)} %bitcast.82), calls=%async_computation.4 | async-start | bytes 5767168
  118.6 11.4 %copy-start.7 = (bf16[2048,768]{0,1:T(8,128)(2,1)S(1)}, bf16[2048,768]{0,1:T(8,128)(2,1)}, u32[]{:S(2)}) copy-start(bf16[2048,768]{0,1:T(8,128)(2,1)} %copy-done.6) | copy-start | bytes 9437188
  118.6 11.3 %copy-start.12 = (bf16[2048,2304]{1,0:T(8,128)(2,1)S(1)}, bf16[2048,2304]{1,0:T(8,128)(2,1)}, u32[]{:S(2)}) copy-start(bf16[2048,2304]{1,0:T(8,128)(2,1)} %get-tuple-element.28) | copy-start | bytes 28311556
  130.0 8.9 %copy-start.5 = (bf16[1,2048,768]{2,1,0:T(8,128)(2,1)S(1)}, bf16[1,2048,768]{2,1,0:T(8,128)(2,1)}, u32[]{:S(2)}) copy-start(bf16[1,2048,768]{2,1,0:T(8,128)(2,1)} %param.12) | copy-start | bytes 9437188
  173.2 19.6 %copy-start.9 = (f32[2048]{0:T(1024)S(1)}, f32[2048]{0:T(1024)}, u32[]{:S(2)}) copy-start(f32[2048]{0:T(1024)} %copy-done.8) | copy-start | bytes 24580
  173.2 19.6 %copy-start.2 = (bf16[1,2048,768]{1,2,0:T(8,128)(2,1)S(1)}, bf16[1,2048,768]{1,2,0:T(8,128)(2,1)}, u32[]{:S(2)}) copy-start(bf16[1,2048,768]{1,2,0:T(8,128)(2,1)} %copy.21) | copy-start | bytes 9437188
  192.8 16.8 %slice-start = ((s8[7077888]{0:T(1024)(128)(4,1)}), s8[4194304]{0:T(1024)(128)(4,1)S(1)}, s32[]{:S(2)}) async-start(s8[7077888]{0:T(1024)(128)(4,1)} %bitcast.80), calls=%async_computation.1 | async-start | bytes 8388608
  198.0 11.6 %slice-start.1 = ((s8[7077888]{0:T(1024)(128)(4,1)}), s8[2883584]{0:T(1024)(128)(4,1)S(1)}, s32[]{:S(2)}) async-start(s8[7077888]{0:T(1024)(128)(4,1)} %bitcast.80), calls=%async_computation.2 | async-start | bytes 5767168
  209.6 10.3 %copy-start.1 = (bf16[1,2048,768]{1,2,0:T(8,128)(2,1)S(1)}, bf16[1,2048,768]{1,2,0:T(8,128)(2,1)}, u32[]{:S(2)}) copy-start(bf16[1,2048,768]{1,2,0:T(8,128)(2,1)} %copy-done) | copy-start | bytes 9437188
  209.6 10.3 %copy-start.11 = (f32[2048]{0:T(1024)S(1)}, f32[2048]{0:T(1024)}, u32[]{:S(2)}) copy-start(f32[2048]{0:T(1024)} %copy-done.10) | copy-start | bytes 24580
  438.0 25.0 %copy-start.3 = (bf16[1,768,2304]{2,1,0:T(8,128)(2,1)S(1)}, bf16[1,768,2304]{2,1,0:T(8,128)(2,1)}, u32[]{:S(2)}) copy-start(bf16[1,768,2304]{2,1,0:T(8,128)(2,1)} %get-tuple-element.9) | copy-start | bytes 10616836
Sparse Core Ops, SparseCore 0:
  255.8 182.0 all-reduce.2
where the time goes:
time: 525 us; the launch traced here: 518 us
  matrix products  232 us (44%)
  waiting for transfers between devices  182 us (35%)
  other arithmetic  78.3 us (15%)
  between operations  14.7 us (3%)
  local copies, waits for them, and re-layouts  9.94 us (2%)
    psum x1, waiting for transfers between devices, step(): summed[number] = [lax.psum(by_w[name], 'dp') for name in NAMES]  182 us
    dot_general x5, matrix products, layer(): gate = jnp.dot(a, w['w_gate'], preferred_element_type=jnp.float32)  84.2 us
    dot_general x5, matrix products, layer(): up = jnp.dot(a, w['w_up'], preferred_element_type=jnp.float32)  84.1 us
    convert_element_type x2, other arithmetic, adamw(): return ((w - 0.02 * step).astype(jnp.bfloat16), m, v)  72.4 us
    dot_general x5, matrix products, matmul(): jnp.dot(a, w, preferred_element_type=jnp.float32).astype(jnp.bfloat16)  64.1 us
  transfers between devices with their start and end apart: 1, of which 1 were waited for; matrix products, arithmetic and copies ran while one was open for 0% of the time, Pallas kernels for 0%

commit v1 on v0

v1 whole, which is shorter than its diff:
```python
import functools

import jax
import jax.numpy as jnp
from jax import lax
from jax.experimental import pallas as pl
from jax.experimental.pallas import tpu as pltpu
from jax.sharding import PartitionSpec as P

F32, BF16 = jnp.float32, jnp.bfloat16
STEPS = 9


class Copy:
    def __init__(self, describe):
        self.describe = describe

    def __getattr__(self, name):
        return getattr(self.describe(), name)


def summed_kernel(side, count, layout, *refs):
    lefts, rights = layout
    n_in = max(lefts) + 1 + count
    left_refs, right_refs, out = refs[: max(lefts) + 1], refs[max(lefts) + 1 : n_in], refs[n_in]
    (lv, rv, other, own, got, b1, b2, ub, cr, fb, l_sem, r_sem, a_s, a_r, b_s, b_r, c_s, c_r, d_s, d_r, e_s, e_r, f_s, f_r, o_sem) = refs[n_in + 1 :]
    rows, half = own.shape[1:]
    chunk, sub = rows // side, rows // side // side
    part = chunk // 2

    me = lax.axis_index("dp")
    core = me % 2
    x, y = me // (2 * side), me // 2 % side
    p1, p2 = x * (1 - core) + y * core, y * (1 - core) + x * core
    far, near = 2 * side * (1 - core) + 2 * core, 2 * (1 - core) + 2 * side * core

    def at(q1, q2):
        return {"dp": q1 * far + q2 * near + core}

    up, down, across = (p1 + 1) % side, (p1 + side - 1) % side, (p1 + 2) % side
    mate = {"dp": me + 1 - 2 * core}
    ups, downs = at(up, p2), at(down, p2)
    others = [at(p1, (p2 + e) % side) for e in range(1, side)]

    barrier = pltpu.get_barrier_semaphore()
    peers = [mate, ups, downs] + others
    for peer in peers:
        pl.semaphore_signal(barrier, inc=1, device_id=peer, device_id_type=pl.DeviceIdType.MESH)
    pl.semaphore_wait(barrier, len(peers))

    mine = pl.ds(pl.multiple_of(core * half, 128), half)
    theirs = pl.ds(pl.multiple_of((1 - core) * half, 128), half)

    def span(start, size):
        return pl.ds(pl.multiple_of(start, 16), size)

    def remote(src, dst, send, recv, to):
        return Copy(
            lambda: pltpu.make_async_remote_copy(
                src_ref=src, dst_ref=dst, send_sem=send, recv_sem=recv, device_id=to, device_id_type=pl.DeviceIdType.MESH
            )
        )

    def copy_a(k):
        return remote(other.at[k % 2], got.at[k], a_s.at[k], a_r.at[k], mate)

    def copies_b(k):
        return (
            remote(got.at[k, span(across * chunk, part)], b1.at[k, 0], b_s.at[k, 0], b_r.at[k, 0], ups),
            remote(got.at[k, span(across * chunk + part, part)], b1.at[k, 1], b_s.at[k, 1], b_r.at[k, 1], downs),
            remote(got.at[k, span(up * chunk + part, part)], b2.at[k, 0, pl.ds(part, part)], b_s.at[k, 2], b_r.at[k, 2], ups),
            remote(got.at[k, span(down * chunk, part)], b2.at[k, 1, pl.ds(0, part)], b_s.at[k, 3], b_r.at[k, 3], downs),
            remote(got.at[k, span(up * chunk, part)], b2.at[k, 0, pl.ds(0, part)], b_s.at[k, 4], b_r.at[k, 4], ups),
            remote(got.at[k, span(down * chunk + part, part)], b2.at[k, 1, pl.ds(part, part)], b_s.at[k, 5], b_r.at[k, 5], downs),
        )

    def copies_c(k):
        return [remote(ub.at[k, e], cr.at[k, e], c_s.at[k, e], c_r.at[k, e], others[e]) for e in range(side - 1)]

    def piece(k, start, size):
        return out.at[k, span(start, size), mine]

    def copies_d(k):
        dst = piece(k, p1 * chunk + p2 * sub, sub)
        return [remote(fb.at[k], dst, d_s.at[k, e], d_r.at[k, e], others[e]) for e in range(side - 1)]

    def copy_o(k):
        return pltpu.make_async_copy(fb.at[k], piece(k, p1 * chunk + p2 * sub, sub), o_sem.at[k])

    def shift(k, start, size, i, to):
        return remote(piece(k, start, size), piece(k, start, size), e_s.at[k, i], e_r.at[k, i], to)

    def copies_e(k):
        return (
            shift(k, p1 * chunk, part, 0, ups),
            shift(k, p1 * chunk + part, part, 1, downs),
            shift(k, p1 * chunk + part, part, 2, ups),
            shift(k, p1 * chunk, part, 3, downs),
            shift(k, down * chunk, part, 4, ups),
            shift(k, up * chunk + part, part, 5, downs),
        )

    def copies_f(k):
        return [
            remote(piece(k, q * chunk, chunk), piece(k, q * chunk, chunk), f_s.at[k, i], f_r.at[k, i], mate)
            for i, q in enumerate((p1, down, up, across))
        ]

    def load(k, which):
        slot = k % 2
        if which == "left":
            return lambda i: pltpu.make_async_copy(left_refs[lefts[i]], lv.at[slot], l_sem.at[slot])
        return lambda i: pltpu.make_async_copy(right_refs[rights[i]].at[:, theirs if which == 0 else mine], rv.at[which], r_sem.at[which])

    def start_load(k, which):
        for i in range(count):

            @pl.when(k == i)
            def _():
                load(k, which)(i).start()

    def dot(k, which, dst):
        block = 256 if rows % 256 == 0 else rows

        def body(j, _):
            r = pl.ds(pl.multiple_of(j * block, block), block)
            dst[r, :] = jnp.dot(lv[k % 2, r, :], rv[which], preferred_element_type=F32).astype(BF16)
            return 0

        lax.fori_loop(0, rows // block, body, 0)

    def add(start, size, dst, *terms):
        def body(j, _):
            total = None
            for ref, first in terms:
                one = ref[span(first + j * sub, sub), :].astype(F32)
                total = one if total is None else total + one
            dst[span(start + j * sub, sub), :] = total.astype(BF16)
            return 0

        lax.fori_loop(0, size // sub, body, 0)

    def step(s, k):
        g, r = own.at[k], got.at[k]
        if s == 0:

            @pl.when(k >= 2)
            def _():
                copy_a(k - 2).wait_send()

            load(k, "left")(0).wait()
            load(k, 0)(0).wait()
            dot(k, 0, other.at[k % 2])
            copy_a(k).start()

            @pl.when(k + 1 < count)
            def _():
                start_load(k + 1, "left")
                start_load(k + 1, 0)

            load(k, 1)(0).wait()
            dot(k, 1, g)

            @pl.when(k + 1 < count)
            def _():
                start_load(k + 1, 1)
        elif s == 1:
            copy_a(k).wait_recv()
            b = copies_b(k)
            add(across * chunk, chunk, r, (g, across * chunk), (r, across * chunk))
            b[0].start()
            b[1].start()
            add(up * chunk + part, part, r, (g, up * chunk + part), (r, up * chunk + part))
            b[2].start()
            add(down * chunk, part, r, (g, down * chunk), (r, down * chunk))
            b[3].start()
        elif s == 2:
            b = copies_b(k)
            b[0].wait_recv()
            add(up * chunk, part, r, (g, up * chunk), (r, up * chunk), (b1.at[k, 0], 0))
            b[4].start()
            b[1].wait_recv()
            add(down * chunk + part, part, r, (g, down * chunk + part), (r, down * chunk + part), (b1.at[k, 1], 0))
            b[5].start()
        elif s == 3:
            for one in copies_b(k)[2:]:
                one.wait_recv()
            for e, one in enumerate(copies_c(k)):
                at_sub = (p2 + e + 1) % side * sub
                first = p1 * chunk + at_sub
                add(0, sub, ub.at[k, e], (g, first), (r, first), (b2.at[k, 0], at_sub), (b2.at[k, 1], at_sub))
                one.start()
        elif s == 4:
            for one in copies_c(k):
                one.wait_recv()
            first = p1 * chunk + p2 * sub
            add(
                0, sub, fb.at[k], (g, first), (r, first), (b2.at[k, 0], p2 * sub), (b2.at[k, 1], p2 * sub),
                *[(cr.at[k, e], 0) for e in range(side - 1)],
            )
            for one in copies_d(k):
                one.start()
            copy_o(k).start()
        elif s == 5:
            copy_o(k).wait()
            for one in copies_d(k):
                one.wait_recv()
            for one in copies_e(k)[:4]:
                one.start()
            copies_f(k)[0].start()
        elif s == 6:
            e = copies_e(k)
            e[0].wait_recv()
            e[4].start()
            e[1].wait_recv()
            e[5].start()
        elif s == 7:
            for one in copies_e(k)[2:]:
                one.wait_recv()
            for one in copies_f(k)[1:]:
                one.start()
        elif s == 8:

            @pl.when(k + 2 >= count)
            def _():
                copy_a(k).wait_send()

            for one in copies_f(k):
                one.wait()
            for one in (*copies_b(k), *copies_c(k), *copies_d(k), *copies_e(k)):
                one.wait_send()

    for which in ("left", 0, 1):
        load(0, which)(0).start()

    def stage(t, _):
        for s in reversed(range(STEPS)):

            @pl.when(jnp.logical_and(t >= s, t - s < count))
            def _():
                step(s, t - s)

        return 0

    lax.fori_loop(0, count + STEPS - 1, stage, 0)


def summed(side, lefts, rights, layout):
    count = len(rights)
    (rows, tokens), columns = lefts[0].shape, rights[0].shape[1]
    half, chunk, sub = columns // 2, rows // side, rows // side // side
    vmem = lambda *shape: pltpu.VMEM(shape, BF16)
    sems = lambda *shape: pltpu.SemaphoreType.DMA(shape)
    hbm = pl.BlockSpec(memory_space=pltpu.HBM)
    return pl.pallas_call(
        functools.partial(summed_kernel, side, count, layout),
        out_shape=jax.ShapeDtypeStruct((count, rows, columns), BF16),
        in_specs=[hbm] * (len(lefts) + count),
        out_specs=hbm,
        scratch_shapes=[
            vmem(2, rows, tokens), vmem(2, tokens, half), vmem(2, rows, half), vmem(count, rows, half), vmem(count, rows, half),
            vmem(count, 2, chunk // 2, half), vmem(count, 2, chunk, half), vmem(count, side - 1, sub, half),
            vmem(count, side - 1, sub, half), vmem(count, sub, half),
            sems(2), sems(2), sems(count), sems(count), sems(count, 6), sems(count, 6), sems(count, side - 1), sems(count, side - 1),
            sems(count, side - 1), sems(count, side - 1), sems(count, 6), sems(count, 6), sems(count, 4), sems(count, 4), sems(count),
        ],
        compiler_params=pltpu.CompilerParams(collective_id=0, has_side_effects=True, vmem_limit_bytes=60 * 2**20),
        cost_estimate=pl.CostEstimate(flops=2 * count * rows * tokens * columns, bytes_accessed=0, transcendentals=0),
        name="summed_gradients",
    )(*lefts, *rights)


def adamw(w, m, v, g):
    m = 0.9 * m + 0.1 * g
    v = 0.95 * v + 0.05 * g * g
    step = m * lax.rsqrt(v + 1e-8) + 0.1 * w
    return (w - 0.02 * step).astype(BF16), m, v


def adamw_kernel(turned, g_ref, w_ref, m_ref, v_ref, ow, om, ov):
    g = g_ref[...].astype(F32)
    ow[...], om[...], ov[...] = adamw(w_ref[...].astype(F32), m_ref[...], v_ref[...], g.T if turned else g)


def adamw_all(places, turned, g, w, m, v):
    layers, rows, columns = w.shape
    block = 96 if not turned else 256
    if layers == 2:
        where = lambda l: places[0] + l * (places[1] - places[0])
    else:
        where = lambda l: sum(jnp.where(l == i, p, 0) for i, p in enumerate(places))
    of = pl.BlockSpec((None, block, columns), lambda l, i: (l, i, 0))
    if turned:
        g_of = pl.BlockSpec((None, columns, block), lambda l, i: (where(l), 0, i))
    else:
        g_of = pl.BlockSpec((None, block, columns), lambda l, i: (where(l), i, 0))
    return pl.pallas_call(
        functools.partial(adamw_kernel, turned),
        grid=(layers, rows // block),
        in_specs=[g_of, of, of, of],
        out_specs=[of] * 3,
        out_shape=[jax.ShapeDtypeStruct(a.shape, a.dtype) for a in (w, m, v)],
        cost_estimate=pl.CostEstimate(flops=layers * rows * columns * 15, bytes_accessed=layers * rows * columns * 22, transcendentals=0),
        name="adamw",
    )(g, w, m, v)


def matmul(a, w, turn=False):
    return lax.dot_general(a, w, (((1,), (1 if turn else 0,)), ((), ())), preferred_element_type=F32)


def normed(h):
    wide = h.astype(F32)
    scale = lax.rsqrt(jnp.mean(wide**2, -1, keepdims=True) + 1e-6)
    return (wide * scale).astype(BF16), wide, scale


def solution(mesh):
    side = int(round((mesh.shape["dp"] // 2) ** 0.5))
    assert side == 4 and 2 * side * side == mesh.shape["dp"]

    def step(x, dy, *arrays):
        (w_gate, w_up, w_down), m, v = (arrays[i : i + 3] for i in (0, 3, 6))
        layers = w_gate.shape[0]
        h, saved = x[0], []
        for l in range(layers):
            a, wide, scale = normed(h)
            gate, up = matmul(a, w_gate[l]), matmul(a, w_up[l])
            sig = jax.nn.sigmoid(gate)
            hidden = (gate * sig * up).astype(BF16)
            saved.append((a, wide, scale, gate, up, sig, hidden))
            if l + 1 < layers:
                h = h + matmul(hidden, w_down[l]).astype(BF16)
        by_h, lefts, rights = dy[0], [], []
        for l in reversed(range(layers)):
            a, wide, scale, gate, up, sig, hidden = saved[l]
            by_hidden = matmul(by_h, w_down[l], True).astype(BF16).astype(F32)
            by_up = (by_hidden * gate * sig).astype(BF16)
            by_gate = (by_hidden * up * (sig + gate * sig * (1 - sig))).astype(BF16)
            lefts += [by_h.T, a.T]
            rights += [hidden, by_gate, by_up]
            if l:
                by_a = matmul(by_gate, w_gate[l], True).astype(BF16) + matmul(by_up, w_up[l], True).astype(BF16)
                by_a = by_a.astype(F32)
                by_wide = scale * by_a - scale**3 * wide * jnp.mean(by_a * wide, -1, keepdims=True)
                by_h = by_h + by_wide.astype(BF16)
        layout = [2 * (i // 3) + (i % 3 > 0) for i in range(3 * layers)], list(range(3 * layers))
        g = summed(side, lefts, rights, layout)
        new = [
            adamw_all([3 * (layers - 1 - l) + i for l in range(layers)], i == 0, g, w, m_, v_)
            for i, w, m_, v_ in ((1, w_gate, m[0], v[0]), (2, w_up, m[1], v[1]), (0, w_down, m[2], v[2]))
        ]
        return tuple(one[which] for which in range(3) for one in new)

    return jax.shard_map(
        step,
        mesh=mesh,
        in_specs=(P(("rep", "dp"), None, None),) * 2 + (P(None, None, None),) * 9,
        out_specs=(P("rep", None, None),) * 9,
        check_vma=False,
    )
```

time: 525 us -> 417 us (0.79)
  Pallas kernels: 0 us -> 244 us
  waiting for transfers between devices: 182 us -> 0 us
  matrix products: 232 us -> 146 us
  other arithmetic: 78.3 us -> 8.04 us
  between operations: 14.7 us -> 1.21 us
    pallas_call x0 -> x4, Pallas kernels: none -> 244 us  [the longest x1 150 us: summed(): pl.pallas_call(functools.partial(summed_kernel, side, count, layout), out...]
    psum x1 -> x0, waiting for transfers between devices: 182 us -> none  [step(): summed[number] = [lax.psum(by_w[name], 'dp') for name in NAMES]]
    dot_general x15 -> x9, matrix products: 232 us -> 146 us  [matmul(): lax.dot_general(a, w, (((1,), (1 if turn else 0,)), ((), ())), preferred_...]
    convert_element_type x2 -> x0, other arithmetic: 72.4 us -> none  [adamw(): return ((w - 0.02 * step).astype(jnp.bfloat16), m, v)]
  transfers between devices with their start and end apart: 1 -> 0, of which waited for: 1 -> 0; matrix products, arithmetic and copies ran while one was open for 0% -> 0% of each run, Pallas kernels for 0% -> 0%
where the time goes in v1:
time: 417 us; the launch traced here: 409 us
  Pallas kernels  244 us (59%)
  matrix products  146 us (35%)
  local copies, waits for them, and re-layouts  9.49 us (2%)
  other arithmetic  8.04 us (2%)
    pallas_call x1, Pallas kernels, summed(): pl.pallas_call(functools.partial(summed_kernel, side, count, layout), out...  150 us
    dot_general x9, matrix products, matmul(): lax.dot_general(a, w, (((1,), (1 if turn else 0,)), ((), ())), preferred_...  146 us
    pallas_call x3, Pallas kernels, adamw_all(): pl.pallas_call(functools.partial(adamw_kernel, turned), grid=(layers, row...  93.8 us
    unnamed x14, local copies, waits for them, and re-layouts  9.49 us

profile of v1, /device:TPU:97, one launch (start us, length us, event | category | flops | bytes accessed | tf_op | source)
XLA Modules:
  0.0 408.8 jit_solution(17871223498320567364)
XLA Ops:
  0.6 3.2 copy.21
  3.8 0.7 fusion.10
  4.5 4.6 %copy.20 = bf16[1,2048,768]{1,2,0:T(8,128)(2,1)} copy(bf16[1,2048,768]{2,1,0:T(8,128)(2,1)} %param.12) | data formatting | bytes 6291456 | tf_op args[1]
  9.2 0.0 copy-start.3
  9.2 12.5 %convolution_convert_fusion.1 = bf16[2048,2304]{1,0:T(8,128)(2,1)} fusion(bf16[2,2304,768]{2,1,0:T(8,128)(2,1)} %w_ref.5, bf16[1,2048,768]{2,1,0:T(8,128)(2,1)} %param.12), kind=kOutput, calls=%fused_computation.17 | convolution fusion | flops 7252475904 | bytes 16121856 | tf_op jit(solution)/shard_map/dot_general | solution.py:309
  21.7 0.0 copy-done.3
  21.7 13.0 %fusion.32 = f32[2048,2304]{1,0:T(8,128)} fusion(bf16[2,768,2304]{2,1,0:T(8,128)(2,1)} %w_ref.3, bf16[1,2048,768]{2,1,0:T(8,128)(2,1)S(1)} %copy-done.3, f32[2048]{0:T(1024)S(1)} %add_rsqrt_fusion.1), kind=kOutput, calls=%fused_computation.50 | convolution fusion | flops 7252475904 | bytes 25567232 | tf_op jit(solution)/shard_map/dot_general | solution.py:309
  34.7 18.9 %multiply_convert_fusion.1 = (bf16[2048,2304]{1,0:T(8,128)(2,1)}, f32[2048,2304]{1,0:T(8,128)}) fusion(f32[2048,2304]{1,0:T(8,128)} %fusion.32, bf16[2,768,2304]{2,1,0:T(8,128)(2,1)} %w_ref.4, bf16[1,2048,768]{2,1,0:T(8,128)(2,1)} %param.11, f32[2048]{0:T(1024)S(1)} %add_rsqrt_fusion.1), kind=kOutput, calls=%fused_computation.14 | convolution fusion | flops 7280787456 | bytes 53878784 | tf_op jit(solution)/shard_map/dot_general | solution.py:309
  53.6 11.8 %fusion.14 = (f32[2048]{0:T(1024)S(1)}, bf16[2048,768]{0,1:T(8,128)(2,1)S(1)}) fusion(bf16[2048,2304]{1,0:T(8,128)(2,1)} %get-tuple-element.36.refs_7_, bf16[2,2304,768]{2,1,0:T(8,128)(2,1)} %w_ref.5, bf16[1,2048,768]{1,2,0:T(8,128)(2,1)S(1)} %copy.21), kind=kOutput, calls=%fused_computation.31 | convolution fusion | flops 7255619584 | bytes 19275776 | tf_op jit(solution)/shard_map/dot_general | solution.py:309
  65.5 0.0 copy-start.1
  65.5 1.6 copy-done.1
  67.2 13.4 %fusion.20 = f32[2048,2304]{1,0:T(8,128)} fusion(bf16[2,768,2304]{2,1,0:T(8,128)(2,1)} %w_ref.3, bf16[2048,768]{0,1:T(8,128)(2,1)S(1)} %get-tuple-element.39, f32[2048]{0:T(1024)S(1)} %get-tuple-element.35), kind=kOutput, calls=%fused_computation.38 | convolution fusion | flops 7252475904 | bytes 25567232 | tf_op jit(solution)/shard_map/dot_general | solution.py:309
  80.5 31.3 %multiply_convert_fusion = (bf16[2048,2304]{1,0:T(8,128)(2,1)}, bf16[2048,2304]{1,0:T(8,128)(2,1)}, bf16[2048,2304]{1,0:T(8,128)(2,1)}) fusion(f32[2048,2304]{1,0:T(8,128)} %fusion.20, bf16[2048,2304]{1,0:T(8,128)(2,1)} %convolution_convert_fusion.1, bf16[2,768,2304]{2,1,0:T(8,128)(2,1)} %w_ref.4, bf16[2048,768]{0,1:T(8,128)(2,1)} %copy-done.1, ...), kind=kOutput, calls=%fused_computation.12 | convolution fusion | flops 7327973376 | bytes 63315968 | tf_op jit(solution)/shard_map/dot_general | solution.py:309
  111.8 0.0 copy-start.5
  111.8 11.3 %fusion.40 = bf16[2048,768]{0,1:T(8,128)(2,1)S(1)} fusion(bf16[2048,2304]{1,0:T(8,128)(2,1)} %get-tuple-element.29.refs_6_, bf16[2,768,2304]{2,1,0:T(8,128)(2,1)} %w_ref.4), kind=kOutput, calls=%fused_computation.56 | convolution fusion | flops 7249330176 | bytes 16121856 | tf_op jit(solution)/shard_map/dot_general | solution.py:309
  123.1 0.0 copy-done.5
  123.1 0.0 copy-start.2
  123.2 9.4 %fusion.56 = bf16[2048,768]{0,1:T(8,128)(2,1)S(1)} fusion(bf16[2048,768]{0,1:T(8,128)(2,1)S(1)} %fusion.40, bf16[2048,2304]{1,0:T(8,128)(2,1)S(1)} %copy-done.5, bf16[2,768,2304]{2,1,0:T(8,128)(2,1)} %w_ref.3), kind=kOutput, calls=%fused_computation.69 | convolution fusion | flops 7250903040 | bytes 19267584 | tf_op jit(solution)/shard_map/dot_general | solution.py:309
  132.6 0.0 copy-done.2
  132.6 0.0 copy-start
  132.6 4.8 %fusion.17 = (f32[2048]{0:T(1024)S(1)}, bf16[768,2048]{1,0:T(8,128)(2,1)}, bf16[768,2048]{1,0:T(8,128)(2,1)}) fusion(bf16[2048,768]{0,1:T(8,128)(2,1)S(1)} %copy-done.2, bf16[2048,768]{0,1:T(8,128)(2,1)S(1)} %fusion.56, f32[2048]{0:T(1024)S(1)} %get-tuple-element.35, f32[2048]{0:T(1024)S(1)} %add_rsqrt_fusion.1, bf16[1,2048,768]{1,2,0:T(8,128)(2,1)S(1)} %copy.21), kind=kLoop, calls=%fused_computation.34 | loop fusion | flops 14153728 | bytes 15753216 | tf_op jit(solution)/shard_map/reduce_sum | solution.py:345
  137.4 0.0 copy-done
  137.4 2.6 fusion.47
  140.0 0.0 copy-start.4
  140.0 24.8 %fusion.7 = (bf16[2048,2304]{1,0:T(8,128)(2,1)}, bf16[2048,2304]{1,0:T(8,128)(2,1)}) fusion(f32[2048,2304]{1,0:T(8,128)} %fusion.32, f32[2048,2304]{1,0:T(8,128)} %get-tuple-element.37, bf16[2048,768]{0,1:T(8,128)(2,1)S(1)} %fusion.47, bf16[2,2304,768]{2,1,0:T(8,128)(2,1)} %w_ref.5), kind=kOutput, calls=%fused_computation.11 | convolution fusion | flops 7318536192 | bytes 63307776 | tf_op jit(solution)/shard_map/dot_general | solution.py:309
  164.7 0.0 copy-done.4
  164.7 149.8 %summed_gradients.1.g_ref = bf16[6,768,2304]{2,1,0:T(8,128)(2,1)} custom-call(bf16[768,2048]{1,0:T(8,128)(2,1)} %bitcast.68, bf16[768,2048]{1,0:T(8,128)(2,1)} %get-tuple-element.33.refs_1_, bf16[768,2048]{1,0:T(8,128)(2,1)} %bitcast.69, bf16[768,2048]{1,0:T(8,128)(2,1)} %get-tuple-element.40.refs_3_, bf16[2048,2304]{1,0:T(8,128)(2,1)} %get-tuple-element.27.refs_4_, ...), custom_call_target="tpu_custom_call" | custom-call | flops 43486543872 | tf_op jit(solution)/shard_map/summed_gradients/pallas_call | solution.py:255
  314.5 32.8 %adamw.5 = (bf16[2,2304,768]{2,1,0:T(8,128)(2,1)}, f32[2,2304,768]{2,1,0:T(8,128)}, f32[2,2304,768]{2,1,0:T(8,128)}) custom-call(bf16[6,768,2304]{2,1,0:T(8,128)(2,1)} %summed_gradients.1.g_ref, bf16[2,2304,768]{2,1,0:T(8,128)(2,1)} %w_ref.5, f32[2,2304,768]{2,1,0:T(8,128)} %m_ref.5, f32[2,2304,768]{2,1,0:T(8,128)} %v_ref.5), custom_call_target="tpu_custom_call" | custom-call | flops 53084160 | bytes 77856768 | tf_op jit(solution)/shard_map/adamw/pallas_call | solution.py:297
  347.3 30.5 %adamw.4 = (bf16[2,768,2304]{2,1,0:T(8,128)(2,1)}, f32[2,768,2304]{2,1,0:T(8,128)}, f32[2,768,2304]{2,1,0:T(8,128)}) custom-call(bf16[6,768,2304]{2,1,0:T(8,128)(2,1)} %summed_gradients.1.g_ref, bf16[2,768,2304]{2,1,0:T(8,128)(2,1)} %w_ref.4, f32[2,768,2304]{2,1,0:T(8,128)} %m_ref.4, f32[2,768,2304]{2,1,0:T(8,128)} %v_ref.4), custom_call_target="tpu_custom_call" | custom-call | flops 53084160 | bytes 77856768 | tf_op jit(solution)/shard_map/adamw/pallas_call | solution.py:297
  377.8 30.5 %adamw.3 = (bf16[2,768,2304]{2,1,0:T(8,128)(2,1)}, f32[2,768,2304]{2,1,0:T(8,128)}, f32[2,768,2304]{2,1,0:T(8,128)}) custom-call(bf16[6,768,2304]{2,1,0:T(8,128)(2,1)} %summed_gradients.1.g_ref, bf16[2,768,2304]{2,1,0:T(8,128)(2,1)} %w_ref.3, f32[2,768,2304]{2,1,0:T(8,128)} %m_ref.3, f32[2,768,2304]{2,1,0:T(8,128)} %v_ref.3), custom_call_target="tpu_custom_call" | custom-call | flops 53084160 | bytes 77856768 | tf_op jit(solution)/shard_map/adamw/pallas_call | solution.py:297
  (3 shorter events, 0.0 us)
Async XLA Ops:
  9.2 12.6 %copy-start.3 = (bf16[1,2048,768]{2,1,0:T(8,128)(2,1)S(1)}, bf16[1,2048,768]{2,1,0:T(8,128)(2,1)}, u32[]{:S(2)}) copy-start(bf16[1,2048,768]{2,1,0:T(8,128)(2,1)} %param.11) | copy-start | bytes 9437188
  65.5 1.7 copy-start.1
  111.8 11.3 %copy-start.5 = (bf16[2048,2304]{1,0:T(8,128)(2,1)S(1)}, bf16[2048,2304]{1,0:T(8,128)(2,1)}, u32[]{:S(2)}) copy-start(bf16[2048,2304]{1,0:T(8,128)(2,1)} %get-tuple-element.28.refs_5_) | copy-start | bytes 28311556
  123.1 9.4 %copy-start.2 = (bf16[2048,768]{0,1:T(8,128)(2,1)S(1)}, bf16[2048,768]{0,1:T(8,128)(2,1)}, u32[]{:S(2)}) copy-start(bf16[2048,768]{0,1:T(8,128)(2,1)} %copy-done.1) | copy-start | bytes 9437188
  132.6 4.8 %copy-start = (bf16[1,2048,768]{1,2,0:T(8,128)(2,1)S(1)}, bf16[1,2048,768]{1,2,0:T(8,128)(2,1)}, u32[]{:S(2)}) copy-start(bf16[1,2048,768]{1,2,0:T(8,128)(2,1)} %copy.20) | copy-start | bytes 9437188
  140.0 24.8 %copy-start.4 = (bf16[2048,768]{0,1:T(8,128)(2,1)}, bf16[2048,768]{0,1:T(8,128)(2,1)S(1)}, u32[]{:S(2)}) copy-start(bf16[2048,768]{0,1:T(8,128)(2,1)S(1)} %fusion.47) | copy-start | bytes 9437188

commit v2 on v1

--- a/solution.py
+++ b/solution.py
@@ -26,7 +26,7 @@
     (lv, rv, other, own, got, b1, b2, ub, cr, fb, l_sem, r_sem, a_s, a_r, b_s, b_r, c_s, c_r, d_s, d_r, e_s, e_r, f_s, f_r, o_sem) = refs[n_in + 1 :]
     rows, half = own.shape[1:]
     chunk, sub = rows // side, rows // side // side
-    part = chunk // 2
+    lo, hi = sub, chunk - sub
 
     me = lax.axis_index("dp")
     core = me % 2
@@ -66,12 +66,12 @@
 
     def copies_b(k):
         return (
-            remote(got.at[k, span(across * chunk, part)], b1.at[k, 0], b_s.at[k, 0], b_r.at[k, 0], ups),
-            remote(got.at[k, span(across * chunk + part, part)], b1.at[k, 1], b_s.at[k, 1], b_r.at[k, 1], downs),
-            remote(got.at[k, span(up * chunk + part, part)], b2.at[k, 0, pl.ds(part, part)], b_s.at[k, 2], b_r.at[k, 2], ups),
-            remote(got.at[k, span(down * chunk, part)], b2.at[k, 1, pl.ds(0, part)], b_s.at[k, 3], b_r.at[k, 3], downs),
-            remote(got.at[k, span(up * chunk, part)], b2.at[k, 0, pl.ds(0, part)], b_s.at[k, 4], b_r.at[k, 4], ups),
-            remote(got.at[k, span(down * chunk + part, part)], b2.at[k, 1, pl.ds(part, part)], b_s.at[k, 5], b_r.at[k, 5], downs),
+            remote(got.at[k, span(across * chunk, lo)], b1.at[k, pl.ds(0, lo)], b_s.at[k, 0], b_r.at[k, 0], ups),
+            remote(got.at[k, span(across * chunk + lo, hi)], b1.at[k, pl.ds(lo, hi)], b_s.at[k, 1], b_r.at[k, 1], downs),
+            remote(got.at[k, span(up * chunk + lo, hi)], b2.at[k, 0, pl.ds(lo, hi)], b_s.at[k, 2], b_r.at[k, 2], ups),
+            remote(got.at[k, span(down * chunk, lo)], b2.at[k, 1, pl.ds(0, lo)], b_s.at[k, 3], b_r.at[k, 3], downs),
+            remote(got.at[k, span(up * chunk, lo)], b2.at[k, 0, pl.ds(0, lo)], b_s.at[k, 4], b_r.at[k, 4], ups),
+            remote(got.at[k, span(down * chunk + lo, hi)], b2.at[k, 1, pl.ds(lo, hi)], b_s.at[k, 5], b_r.at[k, 5], downs),
         )
 
     def copies_c(k):
@@ -92,12 +92,12 @@
 
     def copies_e(k):
         return (
-            shift(k, p1 * chunk, part, 0, ups),
-            shift(k, p1 * chunk + part, part, 1, downs),
-            shift(k, p1 * chunk + part, part, 2, ups),
-            shift(k, p1 * chunk, part, 3, downs),
-            shift(k, down * chunk, part, 4, ups),
-            shift(k, up * chunk + part, part, 5, downs),
+            shift(k, p1 * chunk, lo, 0, ups),
+            shift(k, p1 * chunk + lo, hi, 1, downs),
+            shift(k, p1 * chunk + lo, hi, 2, ups),
+            shift(k, p1 * chunk, lo, 3, downs),
+            shift(k, down * chunk, lo, 4, ups),
+            shift(k, up * chunk + lo, hi, 5, downs),
         )
 
     def copies_f(k):
@@ -170,17 +170,17 @@
             add(across * chunk, chunk, r, (g, across * chunk), (r, across * chunk))
             b[0].start()
             b[1].start()
-            add(up * chunk + part, part, r, (g, up * chunk + part), (r, up * chunk + part))
+            add(up * chunk + lo, hi, r, (g, up * chunk + lo), (r, up * chunk + lo))
             b[2].start()
-            add(down * chunk, part, r, (g, down * chunk), (r, down * chunk))
+            add(down * chunk, lo, r, (g, down * chunk), (r, down * chunk))
             b[3].start()
         elif s == 2:
             b = copies_b(k)
             b[0].wait_recv()
-            add(up * chunk, part, r, (g, up * chunk), (r, up * chunk), (b1.at[k, 0], 0))
+            add(up * chunk, lo, r, (g, up * chunk), (r, up * chunk), (b1.at[k], 0))
             b[4].start()
             b[1].wait_recv()
-            add(down * chunk + part, part, r, (g, down * chunk + part), (r, down * chunk + part), (b1.at[k, 1], 0))
+            add(down * chunk + lo, hi, r, (g, down * chunk + lo), (r, down * chunk + lo), (b1.at[k], lo))
             b[5].start()
         elif s == 3:
             for one in copies_b(k)[2:]:
@@ -259,7 +259,7 @@
         out_specs=hbm,
         scratch_shapes=[
             vmem(2, rows, tokens), vmem(2, tokens, half), vmem(2, rows, half), vmem(count, rows, half), vmem(count, rows, half),
-            vmem(count, 2, chunk // 2, half), vmem(count, 2, chunk, half), vmem(count, side - 1, sub, half),
+            vmem(count, chunk, half), vmem(count, 2, chunk, half), vmem(count, side - 1, sub, half),
             vmem(count, side - 1, sub, half), vmem(count, sub, half),
             sems(2), sems(2), sems(count), sems(count), sems(count, 6), sems(count, 6), sems(count, side - 1), sems(count, side - 1),
             sems(count, side - 1), sems(count, side - 1), sems(count, 6), sems(count, 6), sems(count, 4), sems(count, 4), sems(count),
@@ -277,36 +277,51 @@
     return (w - 0.02 * step).astype(BF16), m, v
 
 
-def adamw_kernel(turned, g_ref, w_ref, m_ref, v_ref, ow, om, ov):
-    g = g_ref[...].astype(F32)
-    ow[...], om[...], ov[...] = adamw(w_ref[...].astype(F32), m_ref[...], v_ref[...], g.T if turned else g)
-
-
-def adamw_all(places, turned, g, w, m, v):
-    layers, rows, columns = w.shape
-    block = 96 if not turned else 256
-    if layers == 2:
-        where = lambda l: places[0] + l * (places[1] - places[0])
-    else:
-        where = lambda l: sum(jnp.where(l == i, p, 0) for i, p in enumerate(places))
-    of = pl.BlockSpec((None, block, columns), lambda l, i: (l, i, 0))
-    if turned:
-        g_of = pl.BlockSpec((None, columns, block), lambda l, i: (where(l), 0, i))
-    else:
-        g_of = pl.BlockSpec((None, block, columns), lambda l, i: (where(l), i, 0))
-    return pl.pallas_call(
+def adamw_kernel(turned, *refs):
+    n = len(turned)
+    for i in range(n):
+        (g, w, m, v), outs = refs[4 * i : 4 * i + 4], refs[4 * n + 3 * i : 4 * n + 3 * i + 3]
+        g = g[...].astype(F32)
+        results = adamw(w[...].astype(F32), m[...], v[...], g.T if turned[i] else g)
+        for out, result in zip(outs, results, strict=True):
+            out[...] = result
+
+
+def adamw_all(g, starts, turned, weights, m, v, parts):
+    layers = weights[0].shape[0]
+    in_specs, out_specs, shapes, operands, bytes_moved = [], [], [], [], 0
+    for i, (w, first) in enumerate(zip(weights, starts, strict=True)):
+        _, rows, columns = w.shape
+        block = rows // parts
+        of = pl.BlockSpec((None, block, columns), lambda l, j: (l, j, 0))
+        if turned[i]:
+            g_of = pl.BlockSpec((None, columns, block), lambda l, j, first=first: (first[0] + first[1] * l, 0, j))
+        else:
+            g_of = pl.BlockSpec((None, block, columns), lambda l, j, first=first: (first[0] + first[1] * l, j, 0))
+        in_specs += [g_of, of, of, of]
+        out_specs += [of] * 3
+        shapes += [jax.ShapeDtypeStruct(a.shape, a.dtype) for a in (w, m[i], v[i])]
+        operands += [g, w, m[i], v[i]]
+        bytes_moved += 22 * layers * rows * columns
+    new = pl.pallas_call(
         functools.partial(adamw_kernel, turned),
-        grid=(layers, rows // block),
-        in_specs=[g_of, of, of, of],
-        out_specs=[of] * 3,
-        out_shape=[jax.ShapeDtypeStruct(a.shape, a.dtype) for a in (w, m, v)],
-        cost_estimate=pl.CostEstimate(flops=layers * rows * columns * 15, bytes_accessed=layers * rows * columns * 22, transcendentals=0),
+        grid=(layers, parts),
+        in_specs=in_specs,
+        out_specs=out_specs,
+        out_shape=shapes,
+        compiler_params=pltpu.CompilerParams(vmem_limit_bytes=60 * 2**20),
+        cost_estimate=pl.CostEstimate(flops=bytes_moved, bytes_accessed=bytes_moved, transcendentals=0),
         name="adamw",
-    )(g, w, m, v)
-
-
-def matmul(a, w, turn=False):
+    )(*operands)
+    return [new[3 * i : 3 * i + 3] for i in range(len(weights))]
+
+
+def dot(a, w, turn=False):
     return lax.dot_general(a, w, (((1,), (1 if turn else 0,)), ((), ())), preferred_element_type=F32)
+
+
+def rounded(value):
+    return value.astype(BF16).astype(F32)
 
 
 def normed(h):
@@ -315,41 +330,100 @@
     return (wide * scale).astype(BF16), wide, scale
 
 
+def local_kernel(x_ref, dy_ref, gate_hbm, up_hbm, down_hbm, *refs):
+    turned, (hidden0, gate0, up0, hidden1, gate1, up1) = refs[:4], refs[4:10]
+    wg, wu, wd, s0, p0, sem = refs[10:]
+    columns = wg.shape[2]
+    block = columns // 3
+    blocks = [pl.ds(j * block, block) for j in range(3)]
+    first = pl.program_id(0) == 0
+
+    def copy(i):
+        source, target = ((gate_hbm, wg), (up_hbm, wu), (down_hbm, wd))[i % 3]
+        return pltpu.make_async_copy(source.at[i // 3], target.at[i // 3], sem.at[i])
+
+    @pl.when(first)
+    def _():
+        for i in range(6):
+            copy(i).start()
+
+    def have(*which):
+        @pl.when(first)
+        def _():
+            for i in which:
+                copy(i).wait()
+
+    dy_turned, a1_turned, dh1_turned, a0_turned = turned
+    x, dy = x_ref[...], dy_ref[...]
+    a0, _, _ = normed(x)
+    a0_turned[...] = a0.T
+    dy_turned[...] = dy.T
+    have(0, 1)
+    for c in blocks:
+        gate, up = dot(a0, wg[0, :, c]), dot(a0, wu[0, :, c])
+        sig = jax.nn.sigmoid(gate)
+        silu = gate * sig
+        hidden0[:, c] = (silu * up).astype(BF16)
+        s0[:, c] = silu
+        p0[:, c] = up * (sig + silu * (1 - sig))
+    have(2)
+    h = (x.astype(F32) + rounded(dot(hidden0[...], wd[0]))).astype(BF16)
+    a1, wide, scale = normed(h)
+    a1_turned[...] = a1.T
+    have(3, 4, 5)
+    for j, c in enumerate(blocks):
+        gate, up = dot(a1, wg[1, :, c]), dot(a1, wu[1, :, c])
+        by_hidden = rounded(dot(dy, wd[1, c, :], True))
+        sig = jax.nn.sigmoid(gate)
+        silu = gate * sig
+        hidden1[:, c] = (silu * up).astype(BF16)
+        up1[:, c] = (by_hidden * silu).astype(BF16)
+        gate1[:, c] = (by_hidden * up * (sig + silu * (1 - sig))).astype(BF16)
+    by_a = rounded(rounded(dot(gate1[...], wg[1], True)) + rounded(dot(up1[...], wu[1], True)))
+    by_wide = scale * by_a - scale**3 * wide * jnp.mean(by_a * wide, -1, keepdims=True)
+    by_h = (dy.astype(F32) + rounded(by_wide)).astype(BF16)
+    dh1_turned[...] = by_h.T
+    for c in blocks:
+        by_hidden = rounded(dot(by_h, wd[0, c, :], True))
+        up0[:, c] = (by_hidden * s0[:, c]).astype(BF16)
+        gate0[:, c] = (by_hidden * p0[:, c]).astype(BF16)
+
+
+def local(x, dy, w_gate, w_up, w_down):
+    (tokens, d), (layers, _, columns) = x.shape, w_gate.shape
+    assert layers == 2
+    block = min(256, tokens)
+    of = lambda width: pl.BlockSpec((block, width), lambda i: (i, 0))
+    turned = pl.BlockSpec((d, block), lambda i: (0, i))
+    hbm = pl.BlockSpec(memory_space=pltpu.HBM)
+    shape = lambda *s: jax.ShapeDtypeStruct(s, BF16)
+    return pl.pallas_call(
+        local_kernel,
+        grid=(tokens // block,),
+        in_specs=[of(d), of(d), hbm, hbm, hbm],
+        out_specs=[turned] * 4 + [of(columns)] * 6,
+        out_shape=[shape(d, tokens)] * 4 + [shape(tokens, columns)] * 6,
+        scratch_shapes=[pltpu.VMEM(w.shape, BF16) for w in (w_gate, w_up, w_down)]
+        + [pltpu.VMEM((block, columns), F32)] * 2
+        + [pltpu.SemaphoreType.DMA((6,))],
+        compiler_params=pltpu.CompilerParams(vmem_limit_bytes=60 * 2**20),
+        cost_estimate=pl.CostEstimate(flops=18 * tokens * d * columns, bytes_accessed=0, transcendentals=0),
+        name="local_parts",
+    )(x, dy, w_gate, w_up, w_down)
+
+
 def solution(mesh):
     side = int(round((mesh.shape["dp"] // 2) ** 0.5))
     assert side == 4 and 2 * side * side == mesh.shape["dp"]
 
     def step(x, dy, *arrays):
-        (w_gate, w_up, w_down), m, v = (arrays[i : i + 3] for i in (0, 3, 6))
-        layers = w_gate.shape[0]
-        h, saved = x[0], []
-        for l in range(layers):
-            a, wide, scale = normed(h)
-            gate, up = matmul(a, w_gate[l]), matmul(a, w_up[l])
-            sig = jax.nn.sigmoid(gate)
-            hidden = (gate * sig * up).astype(BF16)
-            saved.append((a, wide, scale, gate, up, sig, hidden))
-            if l + 1 < layers:
-                h = h + matmul(hidden, w_down[l]).astype(BF16)
-        by_h, lefts, rights = dy[0], [], []
-        for l in reversed(range(layers)):
-            a, wide, scale, gate, up, sig, hidden = saved[l]
-            by_hidden = matmul(by_h, w_down[l], True).astype(BF16).astype(F32)
-            by_up = (by_hidden * gate * sig).astype(BF16)
-            by_gate = (by_hidden * up * (sig + gate * sig * (1 - sig))).astype(BF16)
-            lefts += [by_h.T, a.T]
-            rights += [hidden, by_gate, by_up]
-            if l:
-                by_a = matmul(by_gate, w_gate[l], True).astype(BF16) + matmul(by_up, w_up[l], True).astype(BF16)
-                by_a = by_a.astype(F32)
-                by_wide = scale * by_a - scale**3 * wide * jnp.mean(by_a * wide, -1, keepdims=True)
-                by_h = by_h + by_wide.astype(BF16)
-        layout = [2 * (i // 3) + (i % 3 > 0) for i in range(3 * layers)], list(range(3 * layers))
-        g = summed(side, lefts, rights, layout)
-        new = [
-            adamw_all([3 * (layers - 1 - l) + i for l in range(layers)], i == 0, g, w, m_, v_)
-            for i, w, m_, v_ in ((1, w_gate, m[0], v[0]), (2, w_up, m[1], v[1]), (0, w_down, m[2], v[2]))
-        ]
+        weights, m, v = (arrays[i : i + 3] for i in (0, 3, 6))
+        layers = weights[0].shape[0]
+        dy_turned, a1_turned, dh1_turned, a0_turned, hidden0, gate0, up0, hidden1, gate1, up1 = local(x[0], dy[0], *weights)
+        lefts = [dy_turned, a1_turned, dh1_turned, a0_turned]
+        g = summed(side, lefts, [hidden1, gate1, up1, hidden0, gate0, up0], ([0, 1, 1, 2, 3, 3], list(range(6))))
+        last = 3 * (layers - 1)
+        new = adamw_all(g, [(last + i, -3) for i in (1, 2, 0)], (False, False, True), weights, m, v, 6)
         return tuple(one[which] for which in range(3) for one in new)
 
     return jax.shard_map(

time: 417 us -> 337 us (0.81); the launches traced: 409 us -> 337 us
  matrix products: 146 us -> 0 us
  Pallas kernels: 244 us -> 336 us
  local copies, waits for them, and re-layouts: 9.49 us -> 0 us
  other arithmetic: 8.04 us -> 0 us
    dot_general x9 -> x0, matrix products: 146 us -> none  [matmul(): lax.dot_general(a, w, (((1,), (1 if turn else 0,)), ((), ())), preferred_...]
    pallas_call x3 -> x2, Pallas kernels: 93.8 us -> 171 us  [the longest x1 94.4 us: local(): pl.pallas_call(local_kernel, grid=(tokens // block,), in_specs=[of(d), of...]
    pallas_call x1, Pallas kernels: 150 us -> 165 us  [summed(): pl.pallas_call(functools.partial(summed_kernel, side, count, layout), out...]
    unnamed x14 -> x0, local copies, waits for them, and re-layouts: 9.49 us -> none
    reduce_sum x2 -> x0, other arithmetic: 5.43 us -> none  [the longest x1 4.76 us: step(): jnp.mean(by_a * wide, -1, keepdims=True)]
where the time goes in v2:
time: 337 us
  Pallas kernels  336 us (100%)
    pallas_call x1, Pallas kernels, summed(): pl.pallas_call(functools.partial(summed_kernel, side, count, layout), out...  165 us
    pallas_call x1, Pallas kernels, local(): pl.pallas_call(local_kernel, grid=(tokens // block,), in_specs=[of(d), of...  94.4 us
    pallas_call x1, Pallas kernels, adamw_all(): pl.pallas_call(functools.partial(adamw_kernel, turned), grid=(layers, par...  76.5 us

profile of v2, /device:TPU:97, one launch (start us, length us, event | category | flops | bytes accessed | tf_op | source)
XLA Modules:
  0.0 336.5 jit_solution(3026839488275644842)
XLA Ops:
  0.6 94.4 %local_parts.1 = (bf16[768,2048]{1,0:T(8,128)(2,1)}, bf16[768,2048]{1,0:T(8,128)(2,1)}, bf16[768,2048]{1,0:T(8,128)(2,1)}, bf16[768,2048]{1,0:T(8,128)(2,1)}, bf...) custom-call(bf16[2048,768]{1,0:T(8,128)(2,1)} %bitcast.2, ...), custom_call_target="tpu_custom_call" | custom-call | flops 65229815808 | tf_op jit(solution)/shard_map/local_parts/pallas_call | solution.py:400
  95.1 164.8 %summed_gradients.1.refs_0_.refs_4_.refs_8_ = bf16[6,768,2304]{2,1,0:T(8,128)(2,1)} custom-call(bf16[768,2048]{1,0:T(8,128)(2,1)} %get-tuple-element.28.refs_0_, bf16[768,2048]{1,0:T(8,128)(2,1)} %get-tuple-element.29.refs_1_, bf16[768,2048]{1,0:T(8,128)(2,1)} %get-tuple-element.30.refs_2_, bf16[768,2048]{1,0:T(8,128)(2,1)} %get-tuple-element.31.refs_3_, ...), custom_call_target="tpu_custom_call" | custom-call | flops 43486543872 | tf_op jit(solution)/shard_map/summed_gradients/pallas_call | solution.py:255
  259.9 76.5 %adamw.1 = (bf16[2,768,2304]{2,1,0:T(8,128)(2,1)}, f32[2,768,2304]{2,1,0:T(8,128)}, f32[2,768,2304]{2,1,0:T(8,128)}, bf16[2,768,2304]{2,1,0:T(8,128)(2,1)}, f32[...) custom-call(bf16[6,768,2304]{2,1,0:T(8,128)(2,1)} %summed_gradients., ...), custom_call_target="tpu_custom_call" | custom-call | flops 233570304 | bytes 233570304 | tf_op jit(solution)/shard_map/adamw/pallas_call | solution.py:306

commit v3 on v2

--- a/solution.py
+++ b/solution.py
@@ -9,6 +9,7 @@
 
 F32, BF16 = jnp.float32, jnp.bfloat16
 STEPS = 9
+SPLIT = 1
 
 
 class Copy:
@@ -19,14 +20,15 @@
         return getattr(self.describe(), name)
 
 
-def summed_kernel(side, count, layout, *refs):
+def summed_kernel(side, gradients, layout, *refs):
     lefts, rights = layout
-    n_in = max(lefts) + 1 + count
+    n_in = max(lefts) + 1 + gradients
+    count = gradients * SPLIT
     left_refs, right_refs, out = refs[: max(lefts) + 1], refs[max(lefts) + 1 : n_in], refs[n_in]
     (lv, rv, other, own, got, b1, b2, ub, cr, fb, l_sem, r_sem, a_s, a_r, b_s, b_r, c_s, c_r, d_s, d_r, e_s, e_r, f_s, f_r, o_sem) = refs[n_in + 1 :]
     rows, half = own.shape[1:]
     chunk, sub = rows // side, rows // side // side
-    lo, hi = sub, chunk - sub
+    lo = hi = chunk // 2
 
     me = lax.axis_index("dp")
     core = me % 2
@@ -42,14 +44,9 @@
     ups, downs = at(up, p2), at(down, p2)
     others = [at(p1, (p2 + e) % side) for e in range(1, side)]
 
-    barrier = pltpu.get_barrier_semaphore()
-    peers = [mate, ups, downs] + others
-    for peer in peers:
-        pl.semaphore_signal(barrier, inc=1, device_id=peer, device_id_type=pl.DeviceIdType.MESH)
-    pl.semaphore_wait(barrier, len(peers))
-
-    mine = pl.ds(pl.multiple_of(core * half, 128), half)
-    theirs = pl.ds(pl.multiple_of((1 - core) * half, 128), half)
+    def columns(k, which):
+        place = k % SPLIT * 2 * half + (core if which else 1 - core) * half
+        return pl.ds(pl.multiple_of(place, 128), half)
 
     def span(start, size):
         return pl.ds(pl.multiple_of(start, 16), size)
@@ -78,7 +75,7 @@
         return [remote(ub.at[k, e], cr.at[k, e], c_s.at[k, e], c_r.at[k, e], others[e]) for e in range(side - 1)]
 
     def piece(k, start, size):
-        return out.at[k, span(start, size), mine]
+        return out.at[k // SPLIT, span(start, size), columns(k, 1)]
 
     def copies_d(k):
         dst = piece(k, p1 * chunk + p2 * sub, sub)
@@ -106,25 +103,25 @@
             for i, q in enumerate((p1, down, up, across))
         ]
 
-    def load(k, which):
-        slot = k % 2
+    def load(k, which, i=0):
         if which == "left":
-            return lambda i: pltpu.make_async_copy(left_refs[lefts[i]], lv.at[slot], l_sem.at[slot])
-        return lambda i: pltpu.make_async_copy(right_refs[rights[i]].at[:, theirs if which == 0 else mine], rv.at[which], r_sem.at[which])
+            slot = k // SPLIT % 2
+            return pltpu.make_async_copy(left_refs[lefts[i]], lv.at[slot], l_sem.at[slot])
+        return pltpu.make_async_copy(right_refs[rights[i]].at[:, columns(k, which)], rv.at[which], r_sem.at[which])
 
     def start_load(k, which):
-        for i in range(count):
-
-            @pl.when(k == i)
-            def _():
-                load(k, which)(i).start()
+        for i in range(gradients):
+
+            @pl.when(k // SPLIT == i)
+            def _():
+                load(k, which, i).start()
 
     def dot(k, which, dst):
         block = 256 if rows % 256 == 0 else rows
 
         def body(j, _):
             r = pl.ds(pl.multiple_of(j * block, block), block)
-            dst[r, :] = jnp.dot(lv[k % 2, r, :], rv[which], preferred_element_type=F32).astype(BF16)
+            dst[r, :] = jnp.dot(lv[k // SPLIT % 2, r, :], rv[which], preferred_element_type=F32).astype(BF16)
             return 0
 
         lax.fori_loop(0, rows // block, body, 0)
@@ -148,17 +145,23 @@
             def _():
                 copy_a(k - 2).wait_send()
 
-            load(k, "left")(0).wait()
-            load(k, 0)(0).wait()
+            @pl.when(k % SPLIT == 0)
+            def _():
+                load(k, "left").wait()
+
+            load(k, 0).wait()
             dot(k, 0, other.at[k % 2])
             copy_a(k).start()
 
+            @pl.when(jnp.logical_and((k + 1) % SPLIT == 0, k + 1 < count))
+            def _():
+                start_load(k + 1, "left")
+
             @pl.when(k + 1 < count)
             def _():
-                start_load(k + 1, "left")
                 start_load(k + 1, 0)
 
-            load(k, 1)(0).wait()
+            load(k, 1).wait()
             dot(k, 1, g)
 
             @pl.when(k + 1 < count)
@@ -231,7 +234,13 @@
                 one.wait_send()
 
     for which in ("left", 0, 1):
-        load(0, which)(0).start()
+        load(0, which).start()
+
+    barrier = pltpu.get_barrier_semaphore()
+    peers = [mate, ups, downs] + others
+    for peer in peers:
+        pl.semaphore_signal(barrier, inc=1, device_id=peer, device_id_type=pl.DeviceIdType.MESH)
+    pl.semaphore_wait(barrier, len(peers))
 
     def stage(t, _):
         for s in reversed(range(STEPS)):
@@ -246,16 +255,17 @@
 
 
 def summed(side, lefts, rights, layout):
-    count = len(rights)
+    gradients = len(rights)
+    count = gradients * SPLIT
     (rows, tokens), columns = lefts[0].shape, rights[0].shape[1]
-    half, chunk, sub = columns // 2, rows // side, rows // side // side
+    half, chunk, sub = columns // SPLIT // 2, rows // side, rows // side // side
     vmem = lambda *shape: pltpu.VMEM(shape, BF16)
     sems = lambda *shape: pltpu.SemaphoreType.DMA(shape)
     hbm = pl.BlockSpec(memory_space=pltpu.HBM)
     return pl.pallas_call(
-        functools.partial(summed_kernel, side, count, layout),
-        out_shape=jax.ShapeDtypeStruct((count, rows, columns), BF16),
-        in_specs=[hbm] * (len(lefts) + count),
+        functools.partial(summed_kernel, side, gradients, layout),
+        out_shape=jax.ShapeDtypeStruct((gradients, rows, columns), BF16),
+        in_specs=[hbm] * (len(lefts) + gradients),
         out_specs=hbm,
         scratch_shapes=[
             vmem(2, rows, tokens), vmem(2, tokens, half), vmem(2, rows, half), vmem(count, rows, half), vmem(count, rows, half),
@@ -265,7 +275,7 @@
             sems(count, side - 1), sems(count, side - 1), sems(count, 6), sems(count, 6), sems(count, 4), sems(count, 4), sems(count),
         ],
         compiler_params=pltpu.CompilerParams(collective_id=0, has_side_effects=True, vmem_limit_bytes=60 * 2**20),
-        cost_estimate=pl.CostEstimate(flops=2 * count * rows * tokens * columns, bytes_accessed=0, transcendentals=0),
+        cost_estimate=pl.CostEstimate(flops=2 * gradients * rows * tokens * columns, bytes_accessed=0, transcendentals=0),
         name="summed_gradients",
     )(*lefts, *rights)
 
@@ -316,6 +326,9 @@
     return [new[3 * i : 3 * i + 3] for i in range(len(weights))]
 
 
+TOKENS = 512
+
+
 def dot(a, w, turn=False):
     return lax.dot_general(a, w, (((1,), (1 if turn else 0,)), ((), ())), preferred_element_type=F32)
 
@@ -331,12 +344,25 @@
 
 
 def local_kernel(x_ref, dy_ref, gate_hbm, up_hbm, down_hbm, *refs):
-    turned, (hidden0, gate0, up0, hidden1, gate1, up1) = refs[:4], refs[4:10]
-    wg, wu, wd, s0, p0, sem = refs[10:]
+    turned, outs, buffers = refs[:4], refs[4:10], refs[10:16]
+    hidden0, gate0, up0, hidden1, gate1, up1 = buffers
+    wg, wu, wd, s0, p0, sem, out_sem = refs[16:]
     columns = wg.shape[2]
     block = columns // 3
     blocks = [pl.ds(j * block, block) for j in range(3)]
-    first = pl.program_id(0) == 0
+    now, steps = pl.program_id(0), pl.num_programs(0)
+    first = now == 0
+    rows = hidden0.shape[0]
+
+    def put(i, step):
+        at = pl.ds(pl.multiple_of(step * rows, 16), rows)
+        return pltpu.make_async_copy(buffers[i], outs[i].at[at], out_sem.at[i])
+
+    def free(*which):
+        @pl.when(now > 0)
+        def _():
+            for i in which:
+                put(i, now - 1).wait()
 
     def copy(i):
         source, target = ((gate_hbm, wg), (up_hbm, wu), (down_hbm, wd))[i % 3]
@@ -359,6 +385,7 @@
     a0_turned[...] = a0.T
     dy_turned[...] = dy.T
     have(0, 1)
+    free(0)
     for c in blocks:
         gate, up = dot(a0, wg[0, :, c]), dot(a0, wu[0, :, c])
         sig = jax.nn.sigmoid(gate)
@@ -366,11 +393,13 @@
         hidden0[:, c] = (silu * up).astype(BF16)
         s0[:, c] = silu
         p0[:, c] = up * (sig + silu * (1 - sig))
+    put(0, now).start()
     have(2)
     h = (x.astype(F32) + rounded(dot(hidden0[...], wd[0]))).astype(BF16)
     a1, wide, scale = normed(h)
     a1_turned[...] = a1.T
     have(3, 4, 5)
+    free(3, 4, 5)
     for j, c in enumerate(blocks):
         gate, up = dot(a1, wg[1, :, c]), dot(a1, wu[1, :, c])
         by_hidden = rounded(dot(dy, wd[1, c, :], True))
@@ -379,20 +408,30 @@
         hidden1[:, c] = (silu * up).astype(BF16)
         up1[:, c] = (by_hidden * silu).astype(BF16)
         gate1[:, c] = (by_hidden * up * (sig + silu * (1 - sig))).astype(BF16)
+    for i in (3, 4, 5):
+        put(i, now).start()
     by_a = rounded(rounded(dot(gate1[...], wg[1], True)) + rounded(dot(up1[...], wu[1], True)))
     by_wide = scale * by_a - scale**3 * wide * jnp.mean(by_a * wide, -1, keepdims=True)
     by_h = (dy.astype(F32) + rounded(by_wide)).astype(BF16)
     dh1_turned[...] = by_h.T
+    free(1, 2)
     for c in blocks:
         by_hidden = rounded(dot(by_h, wd[0, c, :], True))
         up0[:, c] = (by_hidden * s0[:, c]).astype(BF16)
         gate0[:, c] = (by_hidden * p0[:, c]).astype(BF16)
+    put(1, now).start()
+    put(2, now).start()
+
+    @pl.when(now == steps - 1)
+    def _():
+        for i in range(6):
+            put(i, now).wait()
 
 
 def local(x, dy, w_gate, w_up, w_down):
     (tokens, d), (layers, _, columns) = x.shape, w_gate.shape
     assert layers == 2
-    block = min(256, tokens)
+    block = min(TOKENS, tokens)
     of = lambda width: pl.BlockSpec((block, width), lambda i: (i, 0))
     turned = pl.BlockSpec((d, block), lambda i: (0, i))
     hbm = pl.BlockSpec(memory_space=pltpu.HBM)
@@ -401,12 +440,13 @@
         local_kernel,
         grid=(tokens // block,),
         in_specs=[of(d), of(d), hbm, hbm, hbm],
-        out_specs=[turned] * 4 + [of(columns)] * 6,
+        out_specs=[turned] * 4 + [hbm] * 6,
         out_shape=[shape(d, tokens)] * 4 + [shape(tokens, columns)] * 6,
-        scratch_shapes=[pltpu.VMEM(w.shape, BF16) for w in (w_gate, w_up, w_down)]
+        scratch_shapes=[pltpu.VMEM((block, columns), BF16)] * 6
+        + [pltpu.VMEM(w.shape, BF16) for w in (w_gate, w_up, w_down)]
         + [pltpu.VMEM((block, columns), F32)] * 2
-        + [pltpu.SemaphoreType.DMA((6,))],
-        compiler_params=pltpu.CompilerParams(vmem_limit_bytes=60 * 2**20),
+        + [pltpu.SemaphoreType.DMA((6,))] * 2,
+        compiler_params=pltpu.CompilerParams(vmem_limit_bytes=63 * 2**20),
         cost_estimate=pl.CostEstimate(flops=18 * tokens * d * columns, bytes_accessed=0, transcendentals=0),
         name="local_parts",
     )(x, dy, w_gate, w_up, w_down)

time: 337 us -> 317 us (0.941)
  Pallas kernels: 336 us -> 316 us
    pallas_call x1, Pallas kernels: 165 us -> 147 us  [summed(): pl.pallas_call(functools.partial(summed_kernel, side, gradients, layout),...]
where the time goes in v3:
time: 317 us
  Pallas kernels  316 us (100%)
    pallas_call x1, Pallas kernels, summed(): pl.pallas_call(functools.partial(summed_kernel, side, gradients, layout),...  147 us
    pallas_call x1, Pallas kernels, local(): pl.pallas_call(local_kernel, grid=(tokens // block,), in_specs=[of(d), of...  92.8 us
    pallas_call x1, Pallas kernels, adamw_all(): pl.pallas_call(functools.partial(adamw_kernel, turned), grid=(layers, par...  76.5 us

profile of v3, /device:TPU:97, one launch (start us, length us, event | category | flops | bytes accessed | tf_op | source)
XLA Modules:
  0.0 316.7 jit_solution(11860680754516549363)
XLA Ops:
  0.6 92.8 %local_parts.1 = (bf16[768,2048]{1,0:T(8,128)(2,1)}, bf16[768,2048]{1,0:T(8,128)(2,1)}, bf16[768,2048]{1,0:T(8,128)(2,1)}, bf16[768,2048]{1,0:T(8,128)(2,1)}, bf...) custom-call(bf16[2048,768]{1,0:T(8,128)(2,1)} %bitcast.2, ...), custom_call_target="tpu_custom_call" | custom-call | flops 65229815808 | tf_op jit(solution)/shard_map/local_parts/pallas_call | solution.py:439
  93.4 146.6 %summed_gradients.1.refs_0_.refs_4_.refs_8_ = bf16[6,768,2304]{2,1,0:T(8,128)(2,1)} custom-call(bf16[768,2048]{1,0:T(8,128)(2,1)} %get-tuple-element.28.refs_0_, bf16[768,2048]{1,0:T(8,128)(2,1)} %get-tuple-element.29.refs_1_, bf16[768,2048]{1,0:T(8,128)(2,1)} %get-tuple-element.30.refs_2_, bf16[768,2048]{1,0:T(8,128)(2,1)} %get-tuple-element.31.refs_3_, ...), custom_call_target="tpu_custom_call" | custom-call | flops 43486543872 | tf_op jit(solution)/shard_map/summed_gradients/pallas_call | solution.py:265
  240.0 76.5 %adamw.1 = (bf16[2,768,2304]{2,1,0:T(8,128)(2,1)}, f32[2,768,2304]{2,1,0:T(8,128)}, f32[2,768,2304]{2,1,0:T(8,128)}, bf16[2,768,2304]{2,1,0:T(8,128)(2,1)}, f32[...) custom-call(bf16[6,768,2304]{2,1,0:T(8,128)(2,1)} %summed_gradients., ...), custom_call_target="tpu_custom_call" | custom-call | flops 233570304 | bytes 233570304 | tf_op jit(solution)/shard_map/adamw/pallas_call | solution.py:316
